TPU v7x, 32 devices: a whole 2x2x4 slice. The times are simulated.
32 devices in a mesh: batch: 4 (over y, x), seq: 8 (over z, core), section: 1.
Axes of the slice: x: 2, y: 2, z: 4, core: 2. Of those that a mesh axis runs over, the one named last changes fastest.
Arguments:
- acts: bfloat16 [1, 14848, 5120], P('section', ('batch', 'seq')), may hold values from -13 to 13
- cotangent: float32 [1, 14848, 6], P('section', ('batch', 'seq')), may hold values from -120 to 120
- routes: int32 [1, 14848, 6], P('section', ('batch', 'seq')), may hold values from 0 to 159, all different within a row
- router_weight: bfloat16 [1, 5120, 160], P('section', ('batch', 'seq')), may hold values from -0.078125 to 0.078125
Outputs:
- grad_router: float32 [1, 5120, 160], P('section', ('batch', 'seq'))
Inputs may be any that keep to these rules, and one draw needn't show every extreme that they name: `routes`: each token's row names 6 different experts, and every expert is named by some token.
All inputs are finite; a program needn't handle non-finite values.
Results may differ from a plain program's by a relative error of at most 0.0017.
Values may be sent and summed in bfloat16 or wider, within the bound.
A program may use at most 64 MiB of HBM per device.

v0:
```python
import math

import jax
import jax.numpy as jnp
from jax import lax
from jax.sharding import PartitionSpec as P


def shards(acts, cotangent, routes, router_weight):
    layers = acts.shape[0]
    width = acts.shape[2]
    experts = router_weight.shape[2]
    x_part = acts
    logits = jnp.einsum(
        "ltd,lde->lte",
        x_part,
        lax.all_gather(router_weight, ("batch", "seq"), axis=1, tiled=True),
        preferred_element_type=jnp.float32,
    )
    expo = jnp.exp(logits)
    probs = expo / jnp.sum(expo, axis=-1, keepdims=True)
    expert_ids = jnp.arange(experts, dtype=jnp.int32)
    picks = (routes[:, :, :, None] == expert_ids[None, None, None, :]).astype(jnp.float32)
    d_prob = jnp.sum(cotangent[:, :, :, None] * picks, axis=2)
    inner = jnp.sum(probs * d_prob, axis=-1, keepdims=True)
    d_logits = (probs * (d_prob - inner)).astype(jnp.bfloat16)
    x_part = acts
    batch_rows = lax.psum_scatter(
        jnp.einsum("ltd,lte->dle", x_part, d_logits, preferred_element_type=jnp.float32),
        "batch",
        scatter_dimension=0,
        tiled=True,
    )
    summed = lax.psum_scatter(batch_rows, "seq", scatter_dimension=0, tiled=True)
    summed = jnp.transpose(summed, (1, 0, 2))
    local_squares = jnp.sum(summed * summed)
    square_sum = lax.psum(local_squares, ("batch", "seq", "section"))
    entry_count = 1.0 * layers * lax.axis_size("section") * width * experts
    clip_norm = 0.25 * math.sqrt(entry_count)
    clip_scale = jnp.minimum(jnp.float32(1.0), clip_norm / jnp.sqrt(square_sum))
    return summed * clip_scale


def solution(mesh):
    placed = (
        P("section", ("batch", "seq"), None),
        P("section", ("batch", "seq"), None),
        P("section", ("batch", "seq"), None),
        P("section", ("batch", "seq"), None),
    )
    return jax.shard_map(
        shards,
        mesh=mesh,
        in_specs=placed,
        out_specs=P("section", ("batch", "seq"), None),
        check_vma=False,
    )
```

profile of v0, /device:TPU:0, one launch (start us, length us, event | category | flops | bytes accessed | tf_op | source)
XLA Modules:
  0.0 208.4 jit_solution(13384992411788395702)
XLA Ops:
  6.5 0.0 all-gather.2.cloned.1.call-start
  6.5 0.7 all-gather.2.cloned.1.call-update
  7.3 0.0 reduce-scatter.5.cloned.1.call-start
  7.3 0.7 copy.20
  8.0 0.7 copy.21
  8.7 0.3 select_reduce_fusion
  9.0 61.7 %all-gather.2.cloned.1.call-done = bf16[1,5120,160]{2,1,0:T(8,128)(2,1)} async-done(((bf16[1,160,160]{2,1,0:T(8,128)(2,1)}), bf16[1,5120,160]{2,1,0:T(8,128)(2,1)}) %all-gather.2.cloned.1.call-update) | async-done | bytes 1638416 | tf_op jit(solution)/shard_map/all_gather | solution.py:17
  70.7 4.7 %fusion.12 = (f32[464]{0:T(512)S(1)}, f32[464,160]{0,1:T(8,128)S(1)}) fusion(bf16[1,5120,160]{2,1,0:T(8,128)(2,1)} %all-gather.2.cloned.1.call-done, bf16[1,464,5120]{2,1,0:T(8,128)(2,1)} %param.4), kind=kOutput, calls=%fused_computation.18 | convolution fusion | flops 760291392 | bytes 6688576 | tf_op jit(solution)/shard_map/ltd,lde->lte/dot_general | solution.py:14
  75.5 0.1 multiply_reduce_fusion
  75.6 5.1 %convolution_bitcast_fusion = f32[5120,1,160]{0,2,1:T(8,128)} fusion(bf16[1,464,5120]{2,1,0:T(8,128)(2,1)} %param.4, f32[464,160]{0,1:T(8,128)S(1)} %select_reduce_fusion, f32[464]{0:T(512)S(1)} %multiply_reduce_fusion, f32[464,160]{0,1:T(8,128)S(1)} %get-tuple-element.6, f32[464]{0:T(512)S(1)} %get-tuple-element.5), kind=kOutput, calls=%fused_computation | convolution fusion | flops 760514560 | bytes 8625792 | tf_op jit(solution)/shard_map/ltd,lte->dle/dot_general | solution.py:29
  80.6 0.0 reduce-scatter.5.cloned.1.call-update
  80.6 0.0 reduce-scatter.7.cloned.1.call-start
  80.7 43.9 %reduce-scatter.5.cloned.1.call-done = f32[1280,1,160]{0,2,1:T(8,128)} async-done(((f32[5120,1,160]{0,2,1:T(8,128)}), f32[1280,1,160]{0,2,1:T(8,128)}) %reduce-scatter.5.cloned.1.call-update) | async-done | bytes 819216 | tf_op jit(solution)/shard_map/reduce_scatter | solution.py:28
  124.6 2.6 %copy.14 = f32[1280,160]{1,0:T(8,128)} copy(f32[1280,160]{0,1:T(8,128)} %bitcast.37) | data formatting | bytes 1638400
  127.2 0.0 reduce-scatter.7.cloned.1.call-update
  127.2 33.5 %reduce-scatter.7.cloned.1.call-done = f32[160,160]{1,0:T(8,128)} async-done(((f32[1280,160]{1,0:T(8,128)}), f32[160,160]{1,0:T(8,128)}) %reduce-scatter.7.cloned.1.call-update) | async-done | bytes 102416
  160.7 1.0 copy.15
  161.7 0.6 fusion.9
  162.4 38.0 %psum.7 = f32[]{:T(128)} all-reduce(f32[]{:T(128)} %fusion.9), channel_id=1, replica_groups=mesh['batch'=4,'seq'=8,'section'=1] {'batch','seq','section'}, use_global_device_ids=true, to_apply=%region_6.0 | all-reduce | flops 1 | bytes 8 | tf_op jit(solution)/shard_map/psum | solution.py:37
  201.1 0.8 copy.11
  (1 shorter events, 0.0 us)
Async XLA Ops:
  6.5 64.2 %all-gather.2.cloned.1.call-start = ((), (), s32[]{:S(2)}) async-start(), calls=%async_computation.2 | async-start | bytes 2703360 | tf_op jit(solution)/shard_map/all_gather | solution.py:17
  7.3 117.3 %reduce-scatter.5.cloned.1.call-start = ((), (), s32[]{:S(2)}) async-start(), calls=%async_computation.3 | async-start | bytes 4096000 | tf_op jit(solution)/shard_map/reduce_scatter | solution.py:28
  80.6 80.1 %reduce-scatter.7.cloned.1.call-start = ((), (), s32[]{:S(2)}) async-start(), calls=%async_computation.4 | async-start | bytes 1474560
Sparse Core Ops, SparseCore 0:
  10.2 60.5 all-gather.1
  80.8 43.7 reduce-scatter.4
  127.4 33.2 reduce-scatter.6
where the time goes:
time: 210 us; the launch traced here: 208 us
  waiting for transfers between devices  140 us (67%)
  blocking collectives  38 us (18%)
  between operations  13.8 us (7%)
  matrix products  9.79 us (5%)
  local copies, waits for them, and re-layouts  5.82 us (3%)
    all_gather x1, waiting for transfers between devices, shards(): lax.all_gather(router_weight, ('batch', 'seq'), axis=1, tiled=True)  61.7 us
    reduce_scatter x1, waiting for transfers between devices, shards(): lax.psum_scatter(jnp.einsum('ltd,lte->dle', x_part, d_logits, preferred_e...  43.9 us
    psum x1, blocking collectives, shards(): square_sum = lax.psum(local_squares, ('batch', 'seq', 'section'))  38 us
    unnamed x4, waiting for transfers between devices  34.2 us
    dot_general x1, matrix products, shards(): jnp.einsum('ltd,lte->dle', x_part, d_logits, preferred_element_type=jnp.f...  5.06 us
    unnamed x4, local copies, waits for them, and re-layouts  5.05 us
    dot_general x1, matrix products, shards(): jnp.einsum('ltd,lde->lte', x_part, lax.all_gather(router_weight, ('batch'...  4.73 us
  transfers between devices with their start and end apart: 3, of which 3 were waited for; matrix products, arithmetic and copies ran while one was open for 1% of the time, Pallas kernels for 0%

commit v1 on v0

v1 whole, which is shorter than its diff:
```python
import functools
import math

import jax
import jax.numpy as jnp
from jax import lax
from jax.experimental import pallas as pl
from jax.experimental.pallas import tpu as pltpu
from jax.sharding import PartitionSpec as P

MESH = pl.DeviceIdType.MESH
LANES = 128


def shards(acts, cotangent, routes, router_weight):
    layers = acts.shape[0]
    width = acts.shape[2]
    experts = router_weight.shape[2]
    logits = jnp.einsum(
        "ltd,lde->lte",
        acts,
        lax.all_gather(router_weight, ("batch", "seq"), axis=1, tiled=True),
        preferred_element_type=jnp.float32,
    )
    expo = jnp.exp(logits)
    probs = expo / jnp.sum(expo, axis=-1, keepdims=True)
    expert_ids = jnp.arange(experts, dtype=jnp.int32)
    picks = (routes[:, :, :, None] == expert_ids[None, None, None, :]).astype(jnp.float32)
    d_prob = jnp.sum(cotangent[:, :, :, None] * picks, axis=2)
    inner = jnp.sum(probs * d_prob, axis=-1, keepdims=True)
    d_logits = (probs * (d_prob - inner)).astype(jnp.bfloat16)
    batch_rows = lax.psum_scatter(
        jnp.einsum("ltd,lte->dle", acts, d_logits, preferred_element_type=jnp.float32),
        "batch",
        scatter_dimension=0,
        tiled=True,
    )
    summed = lax.psum_scatter(batch_rows, "seq", scatter_dimension=0, tiled=True)
    summed = jnp.transpose(summed, (1, 0, 2))
    square_sum = lax.psum(jnp.sum(summed * summed), ("batch", "seq", "section"))
    entry_count = 1.0 * layers * lax.axis_size("section") * width * experts
    clip_norm = 0.25 * math.sqrt(entry_count)
    clip_scale = jnp.minimum(jnp.float32(1.0), clip_norm / jnp.sqrt(square_sum))
    return summed * clip_scale


def kernel(cfg, acts_hbm, cot_ref, routes_ref, w_ref, out_ref,
           acts_v, wq, wg, logit, dprob, dt, part, rec_c, rec_f, rec_s, rec_l, rec_h,
           quad, flip, sq,
           acts_sem, q_send, q_recv, ag_send, ag_recv, fw_send, fw_recv,
           rs_send, rs_recv, fin_send, fin_recv, sq_send, sq_recv):
    n_batch, n_seq, tokens, width, experts, rows, chunks, clip_norm = cfg
    n_dev = n_batch * n_seq
    quad_cols = 4 * rows
    tail = experts - LANES
    half, quarter = experts // 2, experts // 4
    hrow = rows // 2
    b, s = lax.axis_index("batch"), lax.axis_index("seq")
    y, x = b // 2, b % 2
    z, c = s // 2, s % 2
    zh, zl = z // 2, z % 2
    me = b * n_seq + s
    p_own = zl * 2 + c

    def dev(dy=0, dx=0, dh=0, dl=0, dc=0):
        bb = ((y + dy) % 2) * 2 + (x + dx) % 2
        ss = (((zh + dh) % 2) * 2 + (zl + dl) % 2) * 2 + (c + dc) % 2
        return (bb, ss, 0)

    core, near, far = dev(dc=1), dev(dl=1), dev(dh=1)
    first = dev(dx=1 - c, dy=c)
    second = dev(dx=c, dy=1 - c)

    barrier = pltpu.get_barrier_semaphore()
    for d in range(1, n_dev):
        t = (me + d) % n_dev
        pl.semaphore_signal(barrier, inc=1, device_id=(t // n_seq, t % n_seq, 0), device_id_type=MESH)
    load = pltpu.make_async_copy(acts_hbm, acts_v, acts_sem)
    load.start()
    pl.semaphore_wait(barrier, n_dev - 1)

    sends = []

    def remote(src, dst, ssem, rsem, target):
        copy = pltpu.make_async_remote_copy(
            src_ref=src, dst_ref=dst, send_sem=ssem, recv_sem=rsem,
            device_id=target, device_id_type=MESH)
        copy.start()
        sends.append(copy)
        return copy

    to_core = remote(w_ref, wq.at[p_own], q_send.at[0], q_recv.at[0], core)
    to_near = remote(w_ref, wq.at[p_own], q_send.at[1], q_recv.at[1], near)
    wq[p_own] = w_ref[...]

    lane = lax.broadcasted_iota(jnp.int32, (tokens, 2 * LANES), 1)
    total = jnp.zeros((tokens, 2 * LANES), jnp.float32)
    for k in range(cot_ref.shape[1]):
        total += jnp.where(routes_ref[:, k:k + 1] == lane, cot_ref[:, k:k + 1], 0.0)
    dprob[...] = total

    to_near.wait_recv()
    p_near = (1 - zl) * 2 + c
    relay = remote(wq.at[p_near], wq.at[p_near], q_send.at[2], q_recv.at[2], core)
    to_core.wait_recv()
    relay.wait_recv()

    def slot(df, ds, dz):
        yy = (y + df * c + ds * (1 - c)) % 2
        xx = (x + df * (1 - c) + ds * c) % 2
        return yy * 4 + xx * 2 + (zh + dz) % 2

    own = slot(0, 0, 0)
    for h in range(2):
        rng = slice(h * hrow, (h + 1) * hrow)
        for p in range(4):
            wg[own, h, p] = wq[p, rng, :LANES]
        wg[own, h, 4] = jnp.concatenate([wq[p, rng, LANES:] for p in range(4)], axis=1)

    def ag(src, dst, target):
        at = slot(*src)
        i = dst[0] * 4 + dst[1] * 2 + dst[2]
        return remote(wg.at[at, c], wg.at[at, c], ag_send.at[i], ag_recv.at[i], target)

    def fw(src):
        at = slot(*src)
        i = src[0] * 4 + src[1] * 2 + src[2]
        return remote(wg.at[at, c], wg.at[at, c], fw_send.at[i], fw_recv.at[i], core)

    seg = lax.broadcasted_iota(jnp.int32, (rows, LANES), 1) // tail

    def add_logits(src, fresh=False):
        g = slot(*src)
        a_part = jnp.concatenate([wg[g, h, p] for p in range(4) for h in range(2)], axis=0)
        packed = jnp.concatenate([wg[g, 0, 4], wg[g, 1, 4]], axis=0)
        b_part = jnp.concatenate(
            [jnp.where(seg == p, packed, jnp.zeros_like(packed)) for p in range(4)], axis=0)
        w_part = jnp.concatenate([a_part, b_part], axis=1)
        cols = pl.ds(pl.multiple_of(g * quad_cols, LANES), quad_cols)
        term = jnp.dot(acts_v[:, cols], w_part, preferred_element_type=jnp.float32)
        if fresh:
            logit[...] = term
        else:
            logit[...] += term

    c001 = ag((0, 0, 0), (0, 0, 1), far)
    c100 = ag((0, 0, 0), (1, 0, 0), first)
    c010 = ag((0, 0, 0), (0, 1, 0), second)
    load.wait()
    add_logits((0, 0, 0), fresh=True)
    c100.wait_recv()
    c110 = ag((1, 0, 0), (1, 1, 0), second)
    f100 = fw((1, 0, 0))
    c010.wait_recv()
    f010 = fw((0, 1, 0))
    f100.wait_recv()
    add_logits((0, 1, 0))
    f010.wait_recv()
    add_logits((1, 0, 0))
    c001.wait_recv()
    c101 = ag((0, 0, 1), (1, 0, 1), first)
    c011 = ag((0, 0, 1), (0, 1, 1), second)
    f001 = fw((0, 0, 1))
    c110.wait_recv()
    f110 = fw((1, 1, 0))
    f001.wait_recv()
    add_logits((0, 0, 1))
    f110.wait_recv()
    add_logits((1, 1, 0))
    c101.wait_recv()
    c111 = ag((1, 0, 1), (1, 1, 1), second)
    f101 = fw((1, 0, 1))
    c011.wait_recv()
    f011 = fw((0, 1, 1))
    f101.wait_recv()
    add_logits((0, 1, 1))
    f011.wait_recv()
    add_logits((1, 0, 1))
    c111.wait_recv()
    f111 = fw((1, 1, 1))
    f111.wait_recv()
    add_logits((1, 1, 1))

    tl = logit[:, LANES:]
    folded = tl
    for r in range(1, 4):
        folded = folded + pltpu.roll(tl, r * tail, 1)
    expo_a = jnp.exp(logit[:, :LANES])
    expo_b = jnp.where(lane[:, :LANES] < tail, jnp.exp(folded), 0.0)
    norm = jnp.sum(expo_a + expo_b, axis=1, keepdims=True)
    prob_a, prob_b = expo_a / norm, expo_b / norm
    dp_a, dp_b = dprob[:, :LANES], dprob[:, LANES:]
    inner = jnp.sum(prob_a * dp_a + prob_b * dp_b, axis=1, keepdims=True)
    pad = jnp.zeros((flip.shape[0] - tokens, LANES), jnp.float32)
    for i, value in enumerate((prob_a * (dp_a - inner), prob_b * (dp_b - inner))):
        turned = jnp.transpose(jnp.concatenate([value, pad], axis=0))
        n = LANES if i == 0 else tail
        dt[i * LANES:i * LANES + n, :] = turned[:n, :tokens].astype(jnp.bfloat16)

    def compute(k0, nk):
        for g in range(8):
            gy, gx, gz = g // 4, g // 2 % 2, g % 2
            at = g * quad_cols + k0 * LANES
            value = jnp.dot(dt[...], acts_v[:, at:at + nk * LANES], preferred_element_type=jnp.float32)
            for kk in range(nk):
                for h in range(2):
                    f, e = (gx, gy) if h == 0 else (gy, gx)
                    for q in range(2):
                        r = h * half + q * quarter
                        part[k0 + kk, h, f, e, gz, q] = value[r:r + quarter, kk * LANES:(kk + 1) * LANES]

    fi = x * (1 - c) + y * c
    si = y * (1 - c) + x * c
    n_chunks = len(chunks)

    def rs_start(stage, i):
        k0, nk = chunks[i]
        ks = pl.ds(k0, nk)
        src, dst, target = [
            lambda: (part.at[ks, 1 - c], rec_c.at[ks], core),
            lambda: (part.at[ks, c, 1 - fi], rec_f.at[ks], first),
            lambda: (part.at[ks, c, fi, 1 - si], rec_s.at[ks], second),
            lambda: (part.at[ks, c, fi, si, :, 1 - zl], rec_l.at[ks], near),
            lambda: (part.at[ks, c, fi, si, 1 - zh, zl], rec_h.at[ks], far),
        ][stage]()
        n = stage * n_chunks + i
        return remote(src, dst, rs_send.at[n], rs_recv.at[n], target)

    def rs_finish(stage, i, copy):
        copy.wait_recv()
        k0, nk = chunks[i]
        for k in range(k0, k0 + nk):
            if stage == 0:
                part[k, c] += rec_c[k]
            elif stage == 1:
                part[k, c, fi] += rec_f[k]
            elif stage == 2:
                part[k, c, fi, si] += rec_s[k]
            elif stage == 3:
                for q in range(2):
                    part[k, c, fi, si, q, zl] += rec_l[k, q]
            else:
                part[k, c, fi, si, zh, zl] += rec_h[k]

    flying = {}
    for i in range(n_chunks):
        compute(*chunks[i])
        flying[0, i] = rs_start(0, i)
        if i > 0:
            rs_finish(0, i - 1, flying[0, i - 1])
            flying[1, i - 1] = rs_start(1, i - 1)
    rs_finish(0, n_chunks - 1, flying[0, n_chunks - 1])
    flying[1, n_chunks - 1] = rs_start(1, n_chunks - 1)
    for wave in range(n_chunks + 3):
        for stage in (1, 2, 3, 4):
            i = wave - (stage - 1)
            if 0 <= i < n_chunks:
                rs_finish(stage, i, flying[stage, i])
                if stage < 4:
                    flying[stage + 1, i] = rs_start(stage + 1, i)

    squares = jnp.zeros((quarter, LANES), jnp.float32)
    for k in range(quad_cols // LANES):
        v = part[k, c, fi, si, zh, zl]
        rec_h[k] = v
        squares += v * v
    sq[me] = jnp.broadcast_to(jnp.sum(squares).reshape(1, 1), (1, LANES))
    sq_copies = []
    for d in range(1, n_dev):
        t = (me + d) % n_dev
        sq_copies.append(pltpu.make_async_remote_copy(
            src_ref=sq.at[me], dst_ref=sq.at[me], send_sem=sq_send.at[d], recv_sem=sq_recv.at[d],
            device_id=(t // n_seq, t % n_seq, 0), device_id_type=MESH))
        sq_copies[-1].start()
    q_own = c * 2 + zl
    fins = []
    for n, (dl, dc) in enumerate(((1, 0), (1, 1), (0, 1))):
        p_to = ((zl + dl) % 2) * 2 + (c + dc) % 2
        fins.append(remote(rec_h.at[pl.ds(p_to, 2)], quad.at[q_own], fin_send.at[n], fin_recv.at[n],
                           dev(dl=dl, dc=dc)))
    quad[q_own] = rec_h[pl.ds(p_own, 2)]
    for copy in fins:
        copy.wait_recv()
    for j in range(2):
        block = jnp.concatenate([quad[q, j] for q in range(4)]
                                + [jnp.zeros((2 * LANES - experts, LANES), jnp.float32)], axis=0)
        flip[j * LANES:(j + 1) * LANES, :] = jnp.transpose(block)
    for copy in sq_copies:
        copy.wait()
    total_sq = jnp.sum(jnp.sum(sq[...], axis=0)) * (1.0 / LANES)
    clip_scale = jnp.minimum(jnp.float32(1.0), clip_norm / jnp.sqrt(jnp.full((1, 1), total_sq, jnp.float32)))
    mine = flip[pl.ds(pl.multiple_of(p_own * (rows - LANES), 8), rows), :]
    out_ref[...] = mine[:, :experts] * clip_scale
    for copy in sends:
        copy.wait_send()


def fused(mesh, acts, cotangent, routes, router_weight):
    n_batch, n_seq = mesh.shape["batch"], mesh.shape["seq"]
    layers, tokens, width = acts.shape
    rows, experts = router_weight.shape[1:]
    topk = routes.shape[2]
    quad_tiles = 4 * rows // LANES
    quarter = experts // 4
    chunks = tuple((k, min(2, quad_tiles - k)) for k in range(0, quad_tiles, 2))
    clip_norm = 0.25 * math.sqrt(1.0 * layers * width * experts)
    cfg = (n_batch, n_seq, tokens, width, experts, rows, chunks, clip_norm)
    f32, bf16 = jnp.float32, jnp.bfloat16
    dma = pltpu.SemaphoreType.DMA
    vmem = pl.BlockSpec(memory_space=pltpu.VMEM)
    padded = -(-tokens // LANES) * LANES
    n_dev = n_batch * n_seq
    n_rs = 5 * len(chunks)
    out = pl.pallas_call(
        functools.partial(kernel, cfg),
        out_shape=jax.ShapeDtypeStruct((rows, experts), f32),
        in_specs=[pl.BlockSpec(memory_space=pl.ANY), vmem, vmem, vmem],
        out_specs=vmem,
        scratch_shapes=[
            pltpu.VMEM((tokens, width), bf16),
            pltpu.VMEM((4, rows, experts), bf16),
            pltpu.VMEM((8, 2, 5, rows // 2, LANES), bf16),
            pltpu.VMEM((tokens, 2 * LANES), f32),
            pltpu.VMEM((tokens, 2 * LANES), f32),
            pltpu.VMEM((experts, tokens), bf16),
            pltpu.VMEM((quad_tiles, 2, 2, 2, 2, 2, quarter, LANES), f32),
            pltpu.VMEM((quad_tiles, 2, 2, 2, 2, quarter, LANES), f32),
            pltpu.VMEM((quad_tiles, 2, 2, 2, quarter, LANES), f32),
            pltpu.VMEM((quad_tiles, 2, 2, quarter, LANES), f32),
            pltpu.VMEM((quad_tiles, 2, quarter, LANES), f32),
            pltpu.VMEM((quad_tiles, quarter, LANES), f32),
            pltpu.VMEM((4, 2, quarter, LANES), f32),
            pltpu.VMEM((padded, 2 * LANES), f32),
            pltpu.VMEM((n_dev, 1, LANES), f32),
            dma, dma((3,)), dma((3,)), dma((8,)), dma((8,)), dma((8,)), dma((8,)),
            dma((n_rs,)), dma((n_rs,)), dma((3,)), dma((3,)), dma((n_dev,)), dma((n_dev,)),
        ],
        compiler_params=pltpu.CompilerParams(
            collective_id=0, has_side_effects=True, vmem_limit_bytes=48 * 1024 * 1024),
        name="router_grad",
    )(acts[0], cotangent[0], routes[0], router_weight[0])
    return out[None]


def solution(mesh):
    spec = P("section", ("batch", "seq"), None)

    def step(acts, cotangent, routes, router_weight):
        rows, experts = router_weight.shape[1:]
        cube = (mesh.shape["batch"], mesh.shape["seq"], mesh.shape["section"]) == (4, 8, 1)
        dense = (acts.shape[0] == 1 and LANES < experts == rows and 4 * (experts - LANES) == LANES
                 and 4 * rows == 5 * LANES and acts.shape[1] % 16 == 0)
        if cube and dense:
            return fused(mesh, acts, cotangent, routes, router_weight)
        return shards(acts, cotangent, routes, router_weight)

    return jax.shard_map(step, mesh=mesh, in_specs=(spec,) * 4, out_specs=spec, check_vma=False)
```

time: 210 us -> 67.2 us (0.32)
  waiting for transfers between devices: 140 us -> 0 us
  Pallas kernels: 0 us -> 61.3 us
  blocking collectives: 38 us -> 0 us
  between operations: 13.8 us -> 0.03 us
  matrix products: 9.79 us -> 0 us
    all_gather x1 -> x0, waiting for transfers between devices: 61.7 us -> none  [shards(): lax.all_gather(router_weight, ('batch', 'seq'), axis=1, tiled=True)]
    pallas_call x0 -> x1, Pallas kernels: none -> 61.3 us  [fused(): pl.pallas_call(functools.partial(kernel, cfg), out_shape=jax.ShapeDtypeSt...]
    reduce_scatter x1 -> x0, waiting for transfers between devices: 43.9 us -> none  [shards(): lax.psum_scatter(jnp.einsum('ltd,lte->dle', x_part, d_logits, preferred_e...]
    psum x1 -> x0, blocking collectives: 38 us -> none  [shards(): square_sum = lax.psum(local_squares, ('batch', 'seq', 'section'))]
    unnamed x4 -> x0, waiting for transfers between devices: 34.2 us -> none
    dot_general x2 -> x0, matrix products: 9.79 us -> none  [the longest x1 5.06 us: shards(): jnp.einsum('ltd,lte->dle', x_part, d_logits, preferred_element_type=jnp.f...]
    unnamed x4 -> x7, local copies, waits for them, and re-layouts: 5.05 us -> 5.58 us
  transfers between devices with their start and end apart: 3 -> 0, of which waited for: 3 -> 0; matrix products, arithmetic and copies ran while one was open for 1% -> 0% of each run, Pallas kernels for 0% -> 0%
where the time goes in v1:
time: 67.2 us; the launch traced here: 66.9 us
  Pallas kernels  61.3 us (91%)
  local copies, waits for them, and re-layouts  5.58 us (8%)
    pallas_call x1, Pallas kernels, fused(): pl.pallas_call(functools.partial(kernel, cfg), out_shape=jax.ShapeDtypeSt...  61.3 us
    unnamed x7, local copies, waits for them, and re-layouts  5.58 us

profile of v1, /device:TPU:0, one launch (start us, length us, event | category | flops | bytes accessed | tf_op | source)
XLA Modules:
  0.0 66.9 jit_solution(8286232155309040428)
XLA Ops:
  0.0 0.8 %copy.5 = f32[1,464,6]{2,1,0:T(8,128)S(1)} copy(f32[1,464,6]{1,0,2:T(1,128)} %param.5) | data formatting | bytes 22272 | tf_op args[1]
  0.8 0.8 %copy.6 = s32[1,464,6]{2,1,0:T(8,128)S(1)} copy(s32[1,464,6]{1,0,2:T(1,128)} %param.6) | data formatting | bytes 22272 | tf_op args[2]
  1.7 0.0 copy-start
  1.7 2.3 %copy-done = bf16[1,464,5120]{2,1,0:T(8,128)(2,1)S(1)} copy-done((bf16[1,464,5120]{2,1,0:T(8,128)(2,1)S(1)}, bf16[1,464,5120]{2,1,0:T(8,128)(2,1)}, u32[]{:S(2)}) %copy-start) | copy-done | bytes 4751384
  4.0 0.0 copy-start.1
  4.0 0.9 %copy-done.1 = bf16[1,160,160]{2,1,0:T(8,128)(2,1)S(1)} copy-done((bf16[1,160,160]{2,1,0:T(8,128)(2,1)S(1)}, bf16[1,160,160]{2,1,0:T(8,128)(2,1)}, u32[]{:S(2)}) %copy-start.1) | copy-done | bytes 51224
  4.9 61.3 %router_grad.1 = f32[160,160]{1,0:T(8,128)S(1)} custom-call(bf16[464,5120]{1,0:T(8,128)(2,1)S(1)} %bitcast.5, f32[464,6]{1,0:T(8,128)S(1)} %bitcast.6, s32[464,6]{1,0:T(8,128)S(1)} %bitcast.7, bf16[160,160]{1,0:T(8,128)(2,1)S(1)} %bitcast.9), custom_call_target="tpu_custom_call" | custom-call | tf_op jit(solution)/shard_map/router_grad/pallas_call | solution.py:314
  66.2 0.7 %copy.8 = f32[1,160,160]{2,1,0:T(8,128)} copy(f32[1,160,160]{2,1,0:T(8,128)S(1)} %bitcast.8) | data formatting | bytes 204800
Async XLA Ops:
  1.7 2.4 %copy-start = (bf16[1,464,5120]{2,1,0:T(8,128)(2,1)S(1)}, bf16[1,464,5120]{2,1,0:T(8,128)(2,1)}, u32[]{:S(2)}) copy-start(bf16[1,464,5120]{2,1,0:T(8,128)(2,1)} %param.4) | copy-start | bytes 14254084
  4.0 0.9 %copy-start.1 = (bf16[1,160,160]{2,1,0:T(8,128)(2,1)S(1)}, bf16[1,160,160]{2,1,0:T(8,128)(2,1)}, u32[]{:S(2)}) copy-start(bf16[1,160,160]{2,1,0:T(8,128)(2,1)} %param.7) | copy-start | bytes 153604

commit v2 on v1

--- a/solution.py
+++ b/solution.py
@@ -44,10 +44,10 @@
     return summed * clip_scale
 
 
-def kernel(cfg, acts_hbm, cot_ref, routes_ref, w_ref, out_ref,
-           acts_v, wq, wg, logit, dprob, dt, part, rec_c, rec_f, rec_s, rec_l, rec_h,
+def kernel(cfg, acts_hbm, cot_hbm, routes_hbm, w_hbm, out_ref,
+           acts_v, cot_ref, routes_ref, wq, wg, logit, dprob, dt, part, low, rec_c, rec_f, rec_s, rec_l, rec_h,
            quad, flip, sq,
-           acts_sem, q_send, q_recv, ag_send, ag_recv, fw_send, fw_recv,
+           load_sem, q_send, q_recv, ag_send, ag_recv, fw_send, fw_recv,
            rs_send, rs_recv, fin_send, fin_recv, sq_send, sq_recv):
     n_batch, n_seq, tokens, width, experts, rows, chunks, clip_norm = cfg
     n_dev = n_batch * n_seq
@@ -72,12 +72,14 @@
     second = dev(dx=c, dy=1 - c)
 
     barrier = pltpu.get_barrier_semaphore()
-    for d in range(1, n_dev):
-        t = (me + d) % n_dev
-        pl.semaphore_signal(barrier, inc=1, device_id=(t // n_seq, t % n_seq, 0), device_id_type=MESH)
-    load = pltpu.make_async_copy(acts_hbm, acts_v, acts_sem)
-    load.start()
-    pl.semaphore_wait(barrier, n_dev - 1)
+    for target in (core, near, far, first, second):
+        pl.semaphore_signal(barrier, inc=1, device_id=target, device_id_type=MESH)
+    loads = [pltpu.make_async_copy(src, dst, load_sem.at[i]) for i, (src, dst) in enumerate((
+        (w_hbm, wq.at[p_own]), (cot_hbm, cot_ref), (routes_hbm, routes_ref), (acts_hbm, acts_v)))]
+    for load in loads:
+        load.start()
+    loads[0].wait()
+    pl.semaphore_wait(barrier, 5)
 
     sends = []
 
@@ -89,14 +91,15 @@
         sends.append(copy)
         return copy
 
-    to_core = remote(w_ref, wq.at[p_own], q_send.at[0], q_recv.at[0], core)
-    to_near = remote(w_ref, wq.at[p_own], q_send.at[1], q_recv.at[1], near)
-    wq[p_own] = w_ref[...]
-
-    lane = lax.broadcasted_iota(jnp.int32, (tokens, 2 * LANES), 1)
-    total = jnp.zeros((tokens, 2 * LANES), jnp.float32)
-    for k in range(cot_ref.shape[1]):
-        total += jnp.where(routes_ref[:, k:k + 1] == lane, cot_ref[:, k:k + 1], 0.0)
+    to_core = remote(wq.at[p_own], wq.at[p_own], q_send.at[0], q_recv.at[0], core)
+    to_near = remote(wq.at[p_own], wq.at[p_own], q_send.at[1], q_recv.at[1], near)
+
+    loads[1].wait()
+    loads[2].wait()
+    expert = lax.broadcasted_iota(jnp.int32, (experts, tokens), 0)
+    total = jnp.zeros((experts, tokens), jnp.float32)
+    for k in range(cot_ref.shape[0]):
+        total += jnp.where(routes_ref[k] == expert, cot_ref[k], 0.0)
     dprob[...] = total
 
     to_near.wait_recv()
@@ -117,15 +120,19 @@
             wg[own, h, p] = wq[p, rng, :LANES]
         wg[own, h, 4] = jnp.concatenate([wq[p, rng, LANES:] for p in range(4)], axis=1)
 
-    def ag(src, dst, target):
+    pieces = ((0, 2), (2, 3))
+
+    def gather(src, dst, i, target):
         at = slot(*src)
-        i = dst[0] * 4 + dst[1] * 2 + dst[2]
-        return remote(wg.at[at, c], wg.at[at, c], ag_send.at[i], ag_recv.at[i], target)
-
-    def fw(src):
+        n = (dst[0] * 4 + dst[1] * 2 + dst[2]) * 2 + i
+        ref = wg.at[at, c, pl.ds(*pieces[i])]
+        return remote(ref, ref, ag_send.at[n], ag_recv.at[n], target)
+
+    def fw(src, i):
         at = slot(*src)
-        i = src[0] * 4 + src[1] * 2 + src[2]
-        return remote(wg.at[at, c], wg.at[at, c], fw_send.at[i], fw_recv.at[i], core)
+        n = (src[0] * 4 + src[1] * 2 + src[2]) * 2 + i
+        ref = wg.at[at, c, pl.ds(*pieces[i])]
+        return remote(ref, ref, fw_send.at[n], fw_recv.at[n], core)
 
     seg = lax.broadcasted_iota(jnp.int32, (rows, LANES), 1) // tail
 
@@ -143,59 +150,52 @@
         else:
             logit[...] += term
 
-    c001 = ag((0, 0, 0), (0, 0, 1), far)
-    c100 = ag((0, 0, 0), (1, 0, 0), first)
-    c010 = ag((0, 0, 0), (0, 1, 0), second)
-    load.wait()
+    got, given = {}, {}
+    for i in range(2):
+        for dst, target in (((0, 0, 1), far), ((1, 0, 0), first), ((0, 1, 0), second)):
+            got[dst, i] = gather((0, 0, 0), dst, i, target)
+    loads[3].wait()
     add_logits((0, 0, 0), fresh=True)
-    c100.wait_recv()
-    c110 = ag((1, 0, 0), (1, 1, 0), second)
-    f100 = fw((1, 0, 0))
-    c010.wait_recv()
-    f010 = fw((0, 1, 0))
-    f100.wait_recv()
-    add_logits((0, 1, 0))
-    f010.wait_recv()
-    add_logits((1, 0, 0))
-    c001.wait_recv()
-    c101 = ag((0, 0, 1), (1, 0, 1), first)
-    c011 = ag((0, 0, 1), (0, 1, 1), second)
-    f001 = fw((0, 0, 1))
-    c110.wait_recv()
-    f110 = fw((1, 1, 0))
-    f001.wait_recv()
-    add_logits((0, 0, 1))
-    f110.wait_recv()
-    add_logits((1, 1, 0))
-    c101.wait_recv()
-    c111 = ag((1, 0, 1), (1, 1, 1), second)
-    f101 = fw((1, 0, 1))
-    c011.wait_recv()
-    f011 = fw((0, 1, 1))
-    f101.wait_recv()
-    add_logits((0, 1, 1))
-    f011.wait_recv()
-    add_logits((1, 0, 1))
-    c111.wait_recv()
-    f111 = fw((1, 1, 1))
-    f111.wait_recv()
-    add_logits((1, 1, 1))
-
-    tl = logit[:, LANES:]
-    folded = tl
-    for r in range(1, 4):
-        folded = folded + pltpu.roll(tl, r * tail, 1)
-    expo_a = jnp.exp(logit[:, :LANES])
-    expo_b = jnp.where(lane[:, :LANES] < tail, jnp.exp(folded), 0.0)
-    norm = jnp.sum(expo_a + expo_b, axis=1, keepdims=True)
-    prob_a, prob_b = expo_a / norm, expo_b / norm
-    dp_a, dp_b = dprob[:, :LANES], dprob[:, LANES:]
-    inner = jnp.sum(prob_a * dp_a + prob_b * dp_b, axis=1, keepdims=True)
+
+    def arrive(src, i, onward=()):
+        got[src, i].wait_recv()
+        for dst, target in onward:
+            got[dst, i] = gather(src, dst, i, target)
+        given[src, i] = fw(src, i)
+
+    def join(src):
+        for i in range(2):
+            given[(src[1], src[0], src[2]), i].wait_recv()
+        add_logits(src)
+
+    for i in range(2):
+        arrive((1, 0, 0), i, [((1, 1, 0), second)])
+        arrive((0, 1, 0), i)
+    for i in range(2):
+        arrive((0, 0, 1), i, [((1, 0, 1), first), ((0, 1, 1), second)])
+        arrive((1, 1, 0), i)
+        if i == 0:
+            join((1, 0, 0))
+            join((0, 1, 0))
+    arrive((1, 0, 1), 0, [((1, 1, 1), second)])
+    arrive((0, 1, 1), 0)
+    join((0, 0, 1))
+    join((1, 1, 0))
+    arrive((1, 0, 1), 1, [((1, 1, 1), second)])
+    arrive((0, 1, 1), 1)
+    arrive((1, 1, 1), 0)
+    join((1, 0, 1))
+    join((0, 1, 1))
+    arrive((1, 1, 1), 1)
+    join((1, 1, 1))
+
     pad = jnp.zeros((flip.shape[0] - tokens, LANES), jnp.float32)
-    for i, value in enumerate((prob_a * (dp_a - inner), prob_b * (dp_b - inner))):
-        turned = jnp.transpose(jnp.concatenate([value, pad], axis=0))
-        n = LANES if i == 0 else tail
-        dt[i * LANES:i * LANES + n, :] = turned[:n, :tokens].astype(jnp.bfloat16)
+    turned = [jnp.transpose(jnp.concatenate([logit[:, j:j + LANES], pad], axis=0))[:, :tokens] for j in (0, LANES)]
+    folded = sum(turned[1][r * tail:(r + 1) * tail] for r in range(4))
+    expo = jnp.exp(jnp.concatenate([turned[0], folded], axis=0))
+    probs = expo / jnp.sum(expo, axis=0, keepdims=True)
+    inner = jnp.sum(probs * dprob[...], axis=0, keepdims=True)
+    dt[...] = (probs * (dprob[...] - inner)).astype(jnp.bfloat16)
 
     def compute(k0, nk):
         for g in range(8):
@@ -218,7 +218,7 @@
         ks = pl.ds(k0, nk)
         src, dst, target = [
             lambda: (part.at[ks, 1 - c], rec_c.at[ks], core),
-            lambda: (part.at[ks, c, 1 - fi], rec_f.at[ks], first),
+            lambda: (low.at[ks], rec_f.at[ks], first),
             lambda: (part.at[ks, c, fi, 1 - si], rec_s.at[ks], second),
             lambda: (part.at[ks, c, fi, si, :, 1 - zl], rec_l.at[ks], near),
             lambda: (part.at[ks, c, fi, si, 1 - zh, zl], rec_h.at[ks], far),
@@ -231,9 +231,11 @@
         k0, nk = chunks[i]
         for k in range(k0, k0 + nk):
             if stage == 0:
-                part[k, c] += rec_c[k]
+                part[k, c, fi] += rec_c[k, fi]
+                mail = part[k, c, 1 - fi] + rec_c[k, 1 - fi]
+                low[k] = mail.reshape(low.shape[1:]).astype(jnp.bfloat16)
             elif stage == 1:
-                part[k, c, fi] += rec_f[k]
+                part[k, c, fi] += rec_f[k].astype(jnp.float32).reshape(part.shape[3:])
             elif stage == 2:
                 part[k, c, fi, si] += rec_s[k]
             elif stage == 3:
@@ -306,6 +308,10 @@
     clip_norm = 0.25 * math.sqrt(1.0 * layers * width * experts)
     cfg = (n_batch, n_seq, tokens, width, experts, rows, chunks, clip_norm)
     f32, bf16 = jnp.float32, jnp.bfloat16
+
+    def by_choice(array):
+        return jnp.transpose(array, (2, 0, 1))
+
     dma = pltpu.SemaphoreType.DMA
     vmem = pl.BlockSpec(memory_space=pltpu.VMEM)
     padded = -(-tokens // LANES) * LANES
@@ -314,31 +320,34 @@
     out = pl.pallas_call(
         functools.partial(kernel, cfg),
         out_shape=jax.ShapeDtypeStruct((rows, experts), f32),
-        in_specs=[pl.BlockSpec(memory_space=pl.ANY), vmem, vmem, vmem],
+        in_specs=[pl.BlockSpec(memory_space=pltpu.HBM)] * 4,
         out_specs=vmem,
         scratch_shapes=[
             pltpu.VMEM((tokens, width), bf16),
+            pltpu.VMEM((topk, 1, tokens), f32),
+            pltpu.VMEM((topk, 1, tokens), jnp.int32),
             pltpu.VMEM((4, rows, experts), bf16),
             pltpu.VMEM((8, 2, 5, rows // 2, LANES), bf16),
             pltpu.VMEM((tokens, 2 * LANES), f32),
-            pltpu.VMEM((tokens, 2 * LANES), f32),
+            pltpu.VMEM((experts, tokens), f32),
             pltpu.VMEM((experts, tokens), bf16),
             pltpu.VMEM((quad_tiles, 2, 2, 2, 2, 2, quarter, LANES), f32),
+            pltpu.VMEM((quad_tiles, 2, 2, experts // 2, LANES), bf16),
             pltpu.VMEM((quad_tiles, 2, 2, 2, 2, quarter, LANES), f32),
-            pltpu.VMEM((quad_tiles, 2, 2, 2, quarter, LANES), f32),
+            pltpu.VMEM((quad_tiles, 2, 2, experts // 2, LANES), bf16),
             pltpu.VMEM((quad_tiles, 2, 2, quarter, LANES), f32),
             pltpu.VMEM((quad_tiles, 2, quarter, LANES), f32),
             pltpu.VMEM((quad_tiles, quarter, LANES), f32),
             pltpu.VMEM((4, 2, quarter, LANES), f32),
             pltpu.VMEM((padded, 2 * LANES), f32),
             pltpu.VMEM((n_dev, 1, LANES), f32),
-            dma, dma((3,)), dma((3,)), dma((8,)), dma((8,)), dma((8,)), dma((8,)),
+            dma((4,)), dma((3,)), dma((3,)), dma((16,)), dma((16,)), dma((16,)), dma((16,)),
             dma((n_rs,)), dma((n_rs,)), dma((3,)), dma((3,)), dma((n_dev,)), dma((n_dev,)),
         ],
         compiler_params=pltpu.CompilerParams(
-            collective_id=0, has_side_effects=True, vmem_limit_bytes=48 * 1024 * 1024),
+            collective_id=0, has_side_effects=True, vmem_limit_bytes=67_043_328),
         name="router_grad",
-    )(acts[0], cotangent[0], routes[0], router_weight[0])
+    )(acts[0], by_choice(cotangent), by_choice(routes), router_weight[0])
     return out[None]
 
 

time: 67.2 us -> 55.9 us (0.83)
  Pallas kernels: 61.3 us -> 54.2 us
  local copies, waits for them, and re-layouts: 5.58 us -> 1.59 us
    pallas_call x1, Pallas kernels: 61.3 us -> 54.2 us  [fused(): pl.pallas_call(functools.partial(kernel, cfg), out_shape=jax.ShapeDtypeSt...]
    unnamed x7 -> x1, local copies, waits for them, and re-layouts: 5.58 us -> 1.59 us
where the time goes in v2:
time: 55.9 us; the launch traced here: 55.8 us
  Pallas kernels  54.2 us (97%)
  local copies, waits for them, and re-layouts  1.59 us (3%)
    pallas_call x1, Pallas kernels, fused(): pl.pallas_call(functools.partial(kernel, cfg), out_shape=jax.ShapeDtypeSt...  54.2 us
    unnamed x1, local copies, waits for them, and re-layouts  1.59 us

profile of v2, /device:TPU:0, one launch (start us, length us, event | category | flops | bytes accessed | tf_op | source)
XLA Modules:
  0.0 55.8 jit_solution(16241625836058693454)
XLA Ops:
  0.0 54.2 %router_grad.1 = f32[160,160]{1,0:T(8,128)} custom-call(bf16[464,5120]{1,0:T(8,128)(2,1)} %bitcast.5, f32[6,1,464]{2,1,0:T(1,128)} %bitcast.8, s32[6,1,464]{2,1,0:T(1,128)} %bitcast.9, bf16[160,160]{1,0:T(8,128)(2,1)} %bitcast.7), custom_call_target="tpu_custom_call" | custom-call | tf_op jit(solution)/shard_map/router_grad/pallas_call | solution.py:320
  54.2 1.6 %copy.6 = f32[1,160,160]{2,1,0:T(8,128)} copy(f32[1,160,160]{2,1,0:T(8,128)} %bitcast.6) | data formatting | bytes 204800

commit v3 on v2

--- a/solution.py
+++ b/solution.py
@@ -45,7 +45,7 @@
 
 
 def kernel(cfg, acts_hbm, cot_hbm, routes_hbm, w_hbm, out_ref,
-           acts_v, cot_ref, routes_ref, wq, wg, logit, dprob, dt, part, low, rec_c, rec_f, rec_s, rec_l, rec_h,
+           acts_v, cot_ref, routes_ref, w_own, wq, wg, logit, dprob, dt, part, low, rec_c, rec_f, rec_s, rec_l, rec_h,
            quad, flip, sq,
            load_sem, q_send, q_recv, ag_send, ag_recv, fw_send, fw_recv,
            rs_send, rs_recv, fin_send, fin_recv, sq_send, sq_recv):
@@ -72,14 +72,14 @@
     second = dev(dx=c, dy=1 - c)
 
     barrier = pltpu.get_barrier_semaphore()
-    for target in (core, near, far, first, second):
+    for target in (core, near, dev(dl=1, dc=1), far, first, second):
         pl.semaphore_signal(barrier, inc=1, device_id=target, device_id_type=MESH)
     loads = [pltpu.make_async_copy(src, dst, load_sem.at[i]) for i, (src, dst) in enumerate((
-        (w_hbm, wq.at[p_own]), (cot_hbm, cot_ref), (routes_hbm, routes_ref), (acts_hbm, acts_v)))]
+        (w_hbm, w_own), (cot_hbm, cot_ref), (routes_hbm, routes_ref), (acts_hbm, acts_v)))]
     for load in loads:
         load.start()
     loads[0].wait()
-    pl.semaphore_wait(barrier, 5)
+    pl.semaphore_wait(barrier, 6)
 
     sends = []
 
@@ -91,8 +91,10 @@
         sends.append(copy)
         return copy
 
-    to_core = remote(wq.at[p_own], wq.at[p_own], q_send.at[0], q_recv.at[0], core)
-    to_near = remote(wq.at[p_own], wq.at[p_own], q_send.at[1], q_recv.at[1], near)
+    quad_in = []
+    for n, (target, h) in enumerate(((near, c), (dev(dl=1, dc=1), 1 - c), (core, 1 - c))):
+        quad_in.append(remote(w_own.at[h], wq.at[p_own], q_send.at[n], q_recv.at[n], target))
+    wq[p_own] = w_own[c]
 
     loads[1].wait()
     loads[2].wait()
@@ -102,11 +104,8 @@
         total += jnp.where(routes_ref[k] == expert, cot_ref[k], 0.0)
     dprob[...] = total
 
-    to_near.wait_recv()
-    p_near = (1 - zl) * 2 + c
-    relay = remote(wq.at[p_near], wq.at[p_near], q_send.at[2], q_recv.at[2], core)
-    to_core.wait_recv()
-    relay.wait_recv()
+    for copy in quad_in:
+        copy.wait_recv()
 
     def slot(df, ds, dz):
         yy = (y + df * c + ds * (1 - c)) % 2
@@ -114,23 +113,22 @@
         return yy * 4 + xx * 2 + (zh + dz) % 2
 
     own = slot(0, 0, 0)
-    for h in range(2):
-        rng = slice(h * hrow, (h + 1) * hrow)
-        for p in range(4):
-            wg[own, h, p] = wq[p, rng, :LANES]
-        wg[own, h, 4] = jnp.concatenate([wq[p, rng, LANES:] for p in range(4)], axis=1)
-
-    pieces = ((0, 2), (2, 3))
+    for p in range(4):
+        wg[own, c, p] = wq[p, :, :LANES]
+    wg[own, c, 4] = jnp.concatenate([wq[p, :, LANES:] for p in range(4)], axis=1)
+
+    pieces = ((0, 2), (2, 2), (4, 1))
+    n_pieces = len(pieces)
 
     def gather(src, dst, i, target):
         at = slot(*src)
-        n = (dst[0] * 4 + dst[1] * 2 + dst[2]) * 2 + i
+        n = (dst[0] * 4 + dst[1] * 2 + dst[2]) * n_pieces + i
         ref = wg.at[at, c, pl.ds(*pieces[i])]
         return remote(ref, ref, ag_send.at[n], ag_recv.at[n], target)
 
     def fw(src, i):
         at = slot(*src)
-        n = (src[0] * 4 + src[1] * 2 + src[2]) * 2 + i
+        n = (src[0] * 4 + src[1] * 2 + src[2]) * n_pieces + i
         ref = wg.at[at, c, pl.ds(*pieces[i])]
         return remote(ref, ref, fw_send.at[n], fw_recv.at[n], core)
 
@@ -151,11 +149,11 @@
             logit[...] += term
 
     got, given = {}, {}
-    for i in range(2):
+    for i in range(n_pieces):
         for dst, target in (((0, 0, 1), far), ((1, 0, 0), first), ((0, 1, 0), second)):
             got[dst, i] = gather((0, 0, 0), dst, i, target)
+        given[(0, 0, 0), i] = fw((0, 0, 0), i)
     loads[3].wait()
-    add_logits((0, 0, 0), fresh=True)
 
     def arrive(src, i, onward=()):
         got[src, i].wait_recv()
@@ -164,29 +162,35 @@
         given[src, i] = fw(src, i)
 
     def join(src):
-        for i in range(2):
+        for i in range(n_pieces):
             given[(src[1], src[0], src[2]), i].wait_recv()
-        add_logits(src)
-
-    for i in range(2):
+        add_logits(src, fresh=src == (0, 0, 0))
+
+    join((0, 0, 0))
+    for i in range(n_pieces):
         arrive((1, 0, 0), i, [((1, 1, 0), second)])
         arrive((0, 1, 0), i)
-    for i in range(2):
-        arrive((0, 0, 1), i, [((1, 0, 1), first), ((0, 1, 1), second)])
-        arrive((1, 1, 0), i)
-        if i == 0:
-            join((1, 0, 0))
-            join((0, 1, 0))
+    beyond = [((1, 0, 1), first), ((0, 1, 1), second)]
+    arrive((0, 0, 1), 0, beyond)
+    join((1, 0, 0))
+    join((0, 1, 0))
+    arrive((0, 0, 1), 1, beyond)
+    arrive((1, 1, 0), 0)
     arrive((1, 0, 1), 0, [((1, 1, 1), second)])
-    arrive((0, 1, 1), 0)
+    arrive((0, 0, 1), 2, beyond)
+    arrive((1, 1, 0), 1)
+    arrive((1, 1, 0), 2)
+    arrive((1, 0, 1), 1, [((1, 1, 1), second)])
     join((0, 0, 1))
     join((1, 1, 0))
-    arrive((1, 0, 1), 1, [((1, 1, 1), second)])
-    arrive((0, 1, 1), 1)
+    arrive((1, 0, 1), 2, [((1, 1, 1), second)])
+    for i in range(n_pieces):
+        arrive((0, 1, 1), i)
     arrive((1, 1, 1), 0)
+    arrive((1, 1, 1), 1)
     join((1, 0, 1))
     join((0, 1, 1))
-    arrive((1, 1, 1), 1)
+    arrive((1, 1, 1), 2)
     join((1, 1, 1))
 
     pad = jnp.zeros((flip.shape[0] - tokens, LANES), jnp.float32)
@@ -326,7 +330,8 @@
             pltpu.VMEM((tokens, width), bf16),
             pltpu.VMEM((topk, 1, tokens), f32),
             pltpu.VMEM((topk, 1, tokens), jnp.int32),
-            pltpu.VMEM((4, rows, experts), bf16),
+            pltpu.VMEM((2, rows // 2, experts), bf16),
+            pltpu.VMEM((4, rows // 2, experts), bf16),
             pltpu.VMEM((8, 2, 5, rows // 2, LANES), bf16),
             pltpu.VMEM((tokens, 2 * LANES), f32),
             pltpu.VMEM((experts, tokens), f32),
@@ -341,13 +346,13 @@
             pltpu.VMEM((4, 2, quarter, LANES), f32),
             pltpu.VMEM((padded, 2 * LANES), f32),
             pltpu.VMEM((n_dev, 1, LANES), f32),
-            dma((4,)), dma((3,)), dma((3,)), dma((16,)), dma((16,)), dma((16,)), dma((16,)),
+            dma((4,)), dma((3,)), dma((3,)), dma((24,)), dma((24,)), dma((24,)), dma((24,)),
             dma((n_rs,)), dma((n_rs,)), dma((3,)), dma((3,)), dma((n_dev,)), dma((n_dev,)),
         ],
         compiler_params=pltpu.CompilerParams(
             collective_id=0, has_side_effects=True, vmem_limit_bytes=67_043_328),
         name="router_grad",
-    )(acts[0], by_choice(cotangent), by_choice(routes), router_weight[0])
+    )(acts[0], by_choice(cotangent), by_choice(routes), router_weight.reshape(2, rows // 2, experts))
     return out[None]
 
 

time: 55.9 us -> 56.6 us (1.013)
  Pallas kernels: 54.2 us -> 54.8 us
    pallas_call x1, Pallas kernels: 54.2 us -> 54.8 us  [fused(): pl.pallas_call(functools.partial(kernel, cfg), out_shape=jax.ShapeDtypeSt...]
where the time goes in v3:
time: 56.6 us; the launch traced here: 56.4 us
  Pallas kernels  54.8 us (97%)
  local copies, waits for them, and re-layouts  1.59 us (3%)
    pallas_call x1, Pallas kernels, fused(): pl.pallas_call(functools.partial(kernel, cfg), out_shape=jax.ShapeDtypeSt...  54.8 us
    unnamed x1, local copies, waits for them, and re-layouts  1.59 us

profile of v3, /device:TPU:0, one launch (start us, length us, event | category | flops | bytes accessed | tf_op | source)
XLA Modules:
  0.0 56.4 jit_solution(17785421747255448717)
XLA Ops:
  0.0 54.8 %router_grad.1 = f32[160,160]{1,0:T(8,128)} custom-call(bf16[464,5120]{1,0:T(8,128)(2,1)} %bitcast.5, f32[6,1,464]{2,1,0:T(1,128)} %bitcast.8, s32[6,1,464]{2,1,0:T(1,128)} %bitcast.9, bf16[2,80,160]{2,1,0:T(8,128)(2,1)} %bitcast.7), custom_call_target="tpu_custom_call" | custom-call | tf_op jit(solution)/shard_map/router_grad/pallas_call | solution.py:324
  54.8 1.6 %copy.6 = f32[1,160,160]{2,1,0:T(8,128)} copy(f32[1,160,160]{2,1,0:T(8,128)} %bitcast.6) | data formatting | bytes 204800

commit v4 on v2

--- a/solution.py
+++ b/solution.py
@@ -45,7 +45,7 @@
 
 
 def kernel(cfg, acts_hbm, cot_hbm, routes_hbm, w_hbm, out_ref,
-           acts_v, cot_ref, routes_ref, wq, wg, logit, dprob, dt, part, low, rec_c, rec_f, rec_s, rec_l, rec_h,
+           acts_v, cot_ref, routes_ref, wq, wg, logit, dprob, dt, part, low, low_s, rec_t, rec_c, rec_f, rec_s, rec_l, rec_h,
            quad, flip, sq,
            load_sem, q_send, q_recv, ag_send, ag_recv, fw_send, fw_recv,
            rs_send, rs_recv, fin_send, fin_recv, sq_send, sq_recv):
@@ -219,7 +219,7 @@
         src, dst, target = [
             lambda: (part.at[ks, 1 - c], rec_c.at[ks], core),
             lambda: (low.at[ks], rec_f.at[ks], first),
-            lambda: (part.at[ks, c, fi, 1 - si], rec_s.at[ks], second),
+            lambda: (low_s.at[ks], rec_t.at[ks], second) if i == 0 else (part.at[ks, c, fi, 1 - si], rec_s.at[ks], second),
             lambda: (part.at[ks, c, fi, si, :, 1 - zl], rec_l.at[ks], near),
             lambda: (part.at[ks, c, fi, si, 1 - zh, zl], rec_h.at[ks], far),
         ][stage]()
@@ -236,8 +236,13 @@
                 low[k] = mail.reshape(low.shape[1:]).astype(jnp.bfloat16)
             elif stage == 1:
                 part[k, c, fi] += rec_f[k].astype(jnp.float32).reshape(part.shape[3:])
+                if i == 0:
+                    low_s[k] = part[k, c, fi, 1 - si].reshape(low_s.shape[1:]).astype(jnp.bfloat16)
             elif stage == 2:
-                part[k, c, fi, si] += rec_s[k]
+                if i == 0:
+                    part[k, c, fi, si] += rec_t[k].astype(jnp.float32).reshape(part.shape[4:])
+                else:
+                    part[k, c, fi, si] += rec_s[k]
             elif stage == 3:
                 for q in range(2):
                     part[k, c, fi, si, q, zl] += rec_l[k, q]
@@ -333,6 +338,8 @@
             pltpu.VMEM((experts, tokens), bf16),
             pltpu.VMEM((quad_tiles, 2, 2, 2, 2, 2, quarter, LANES), f32),
             pltpu.VMEM((quad_tiles, 2, 2, experts // 2, LANES), bf16),
+            pltpu.VMEM((chunks[0][1], 2, experts // 2, LANES), bf16),
+            pltpu.VMEM((chunks[0][1], 2, experts // 2, LANES), bf16),
             pltpu.VMEM((quad_tiles, 2, 2, 2, 2, quarter, LANES), f32),
             pltpu.VMEM((quad_tiles, 2, 2, experts // 2, LANES), bf16),
             pltpu.VMEM((quad_tiles, 2, 2, quarter, LANES), f32),

time: 55.9 us -> 55.8 us (level)
  no operation moved by 1% of the time
where the time goes in v4:
time: 55.8 us; the launch traced here: 55.6 us
  Pallas kernels  54 us (97%)
  local copies, waits for them, and re-layouts  1.59 us (3%)
    pallas_call x1, Pallas kernels, fused(): pl.pallas_call(functools.partial(kernel, cfg), out_shape=jax.ShapeDtypeSt...  54 us
    unnamed x1, local copies, waits for them, and re-layouts  1.59 us

profile of v4, /device:TPU:0, one launch (start us, length us, event | category | flops | bytes accessed | tf_op | source)
XLA Modules:
  0.0 55.6 jit_solution(1148833530220103369)
XLA Ops:
  0.0 54.0 %router_grad.1 = f32[160,160]{1,0:T(8,128)} custom-call(bf16[464,5120]{1,0:T(8,128)(2,1)} %bitcast.5, f32[6,1,464]{2,1,0:T(1,128)} %bitcast.8, s32[6,1,464]{2,1,0:T(1,128)} %bitcast.9, bf16[160,160]{1,0:T(8,128)(2,1)} %bitcast.7), custom_call_target="tpu_custom_call" | custom-call | tf_op jit(solution)/shard_map/router_grad/pallas_call | solution.py:325
  54.0 1.6 %copy.6 = f32[1,160,160]{2,1,0:T(8,128)} copy(f32[1,160,160]{2,1,0:T(8,128)} %bitcast.6) | data formatting | bytes 204800
